TPU v7x, 256 devices: a whole 4x4x8 slice. The times are simulated.
256 devices in a mesh: ep: 64 (over x, z, core), dp: 4 (over y).
Axes of the slice: x: 4, y: 4, z: 8, core: 2. Of those that a mesh axis runs over, the one named last changes fastest.
Arguments:
- tokens: bfloat16 [32768, 2048], P(('ep', 'dp')), may hold values from -6 to 6
- routes: int32 [32768, 8], P(('ep', 'dp')), may hold values from 0 to 63, as said below
- gates: bfloat16 [32768, 8], P(('ep', 'dp')), may hold values from 0.19921875 to 1
- w_gate: bfloat16 [64, 2048, 768], P('ep'), may hold values from -0.125 to 0.125
- w_up: bfloat16 [64, 2048, 768], P('ep'), may hold values from -0.125 to 0.125
- w_down: bfloat16 [64, 768, 2048], P('ep'), may hold values from -0.21875 to 0.21875
- score_head: float32 [2048], replicated, may hold values from -0.125 to 0.125
- doc_ids: int32 [256], P(('ep', 'dp')), may hold values from 0 to 63, never falling along the last dimension, each value on 1 to 8 neighbouring positions
Outputs:
- mixed: bfloat16 [32768, 2048], P(('ep', 'dp'))
- doc_scores: float32 [3, 64], replicated
Inputs may be any that keep to these rules, and one draw needn't show every extreme that they name: `routes`: each row names 8 different experts; among the rows of one device no expert is named more than 24 times. `doc_ids`: never falling along the passages; every document has 1 to 8 passages.
All inputs are finite; a program needn't handle non-finite values.
Results may differ from a plain program's by a relative error of at most 0.0058.
Values may be sent and summed in bfloat16 or wider, within the bound.
A program may use at most 64 MiB of HBM per device.

v0:
```python
import math
import jax
import jax.numpy as jnp
from jax import lax
from jax.sharding import Mesh
from jax.sharding import PartitionSpec as P

TOP = 8
PASSAGE = 128
EP = ("x", "z", "core")
EP_DP = ("x", "z", "core", "dp")
CAP = 24


def shards(tokens, routes, gates, w_gate, w_up, w_down, score_head, doc_ids):
    rows, width = tokens.shape
    nx, nz, nc = (lax.axis_size("x"), lax.axis_size("z"), lax.axis_size("core"))
    experts = nx * nz * nc
    hit = routes[:, :, None] == jnp.arange(experts, dtype=jnp.int32)
    routed = hit.any(axis=1)
    gate_of = jnp.where(hit, gates[:, :, None], 0).sum(axis=1)
    below = jnp.tril(jnp.ones((rows, rows), jnp.bfloat16), -1)
    rank = jnp.dot(below, routed.astype(jnp.bfloat16), preferred_element_type=jnp.float32)
    rank = jnp.where(routed, rank, 200.0).astype(jnp.bfloat16)
    packed = jnp.concatenate([tokens, rank, gate_of.astype(jnp.bfloat16)], axis=1)
    held = lax.all_gather(packed, "z")
    mine = lax.axis_index("z")

    def at_z(a):
        a = a.reshape(nz, rows, nx, nz, nc)
        return lax.dynamic_index_in_dim(a, mine, 3, keepdims=False).reshape(nz, rows, nx * nc)

    rank_z = at_z(held[..., width : width + experts])
    gate_z = at_z(held[..., width + experts :])
    slots = jnp.arange(CAP, dtype=jnp.bfloat16)
    chosen = rank_z.transpose(2, 0, 1)[:, :, None, :] == slots[:, None]
    pick = chosen.astype(jnp.bfloat16)
    send = jnp.einsum(
        "dslt,stf->dslf", pick, held[..., :width], preferred_element_type=jnp.bfloat16
    )
    send = send.reshape(nx * nc, nz * CAP, width)
    recv = lax.all_to_all(send, ("x", "core"), split_axis=0, concat_axis=0, tiled=True)
    flat = recv.reshape(-1, width)
    gate_part = jnp.dot(flat, w_gate[0], preferred_element_type=jnp.float32)
    up_part = jnp.dot(flat, w_up[0], preferred_element_type=jnp.float32)
    hidden = (jax.nn.silu(gate_part) * up_part).astype(jnp.bfloat16)
    result = jnp.dot(hidden, w_down[0], preferred_element_type=jnp.float32).astype(jnp.bfloat16)
    back = lax.all_to_all(
        result.reshape(recv.shape), ("x", "core"), split_axis=0, concat_axis=0, tiled=True
    ).reshape(nx * nc, nz, CAP, width)
    mix = jnp.where(chosen, gate_z.transpose(2, 0, 1)[:, :, None, :], 0)
    part = jnp.einsum("dslt,dslf->stf", mix, back, preferred_element_type=jnp.float32)
    mixed = lax.psum_scatter(part.astype(jnp.bfloat16), "z", scatter_dimension=0, tiled=False)
    token_score = jnp.dot(mixed.astype(jnp.float32), score_head, precision=lax.Precision.HIGHEST)
    passage_score = token_score.reshape(-1, PASSAGE).sum(axis=1) / math.sqrt(PASSAGE)
    pair = jnp.stack([passage_score, doc_ids.astype(jnp.float32)], axis=1)
    pairs = lax.all_gather(pair, EP_DP, tiled=True)
    total = pairs.shape[0]
    docs = total // 4
    column = pairs[:, :1]
    member = pairs[:, 1:] == jnp.arange(docs, dtype=jnp.float32)[None, :]
    index = jnp.arange(total, dtype=jnp.int32)[:, None]
    max_score = jnp.where(member, column, -1e30).max(axis=0)
    sum_score = jnp.where(member, column, 0.0).sum(axis=0)
    first = jnp.where(member, index, total).min(axis=0)
    first_score = jnp.where(member & (index == first[None, :]), column, 0.0).sum(axis=0)
    return (mixed, jnp.stack([max_score, first_score, sum_score]))


def solution(mesh):
    finer = Mesh(mesh.devices.reshape(4, 8, 2, mesh.shape["dp"]), EP_DP)
    return jax.shard_map(
        shards,
        mesh=finer,
        in_specs=(
            P(EP_DP, None),
            P(EP_DP, None),
            P(EP_DP, None),
            P(EP, None, None),
            P(EP, None, None),
            P(EP, None, None),
            P(),
            P(EP_DP),
        ),
        out_specs=(P(EP_DP, None), P()),
        check_vma=False,
    )
```

profile of v0, /device:TPU:1, one launch (start us, length us, event | category | flops | bytes accessed | tf_op | source)
XLA Modules:
  0.0 412.3 jit_solution(16684683082836953582)
XLA Ops:
  7.2 0.0 copy-start
  7.2 0.0 all-gather.4.cloned.1.call-start
  7.2 0.9 fusion.14
  8.1 0.2 fusion.10
  8.3 0.1 copy.31
  8.5 0.7 fusion.19
  9.2 0.1 copy.32
  9.3 1.9 concatenate.3
  11.2 0.0 all-gather.4.cloned.1.call-update
  11.2 61.0 %all-gather.4.cloned.1.call-done = bf16[1024,2176]{1,0:T(8,128)(2,1)} async-done(((bf16[128,2176]{1,0:T(8,128)(2,1)}), bf16[1024,2176]{1,0:T(8,128)(2,1)}) %all-gather.4.cloned.1.call-update) | async-done | bytes 4456464 | tf_op jit(solution)/shard_map/all_gather | solution.py:26
  72.2 1.8 fusion.29
  74.0 1.1 copy.33
  75.1 0.8 copy.35
  75.9 0.7 constant_dynamic-slice_fusion
  76.6 4.0 fusion.3
  80.6 1.1 copy.37
  81.7 76.3 %all_to_all.10 = bf16[8,192,2048]{2,1,0:T(8,128)(2,1)S(1)} all-to-all(bf16[8,192,2048]{2,1,0:T(8,128)(2,1)S(1)} %bitcast.54), channel_id=1, replica_groups=mesh['x'=4,'z'=8,'core'=2,'dp'=4] {'x','core'}, dimensions={0} | all-to-all | bytes 12582912 | tf_op jit(solution)/shard_map/all_to_all | solution.py:42
  158.0 5.2 %fusion.8 = f32[1536,768]{1,0:T(8,128)S(1)} fusion(bf16[1536,2048]{1,0:T(8,128)(2,1)S(1)} %bitcast.56, bf16[1,2048,768]{2,1,0:T(8,128)(2,1)S(1)} %copy-done.2), kind=kOutput, calls=%fused_computation.10 | convolution fusion | flops 4831838208 | bytes 14155776 | tf_op jit(solution)/shard_map/dot_general | solution.py:44
  163.2 5.6 %multiply_convert_fusion = bf16[1536,768]{1,0:T(8,128)(2,1)S(1)} fusion(f32[1536,768]{1,0:T(8,128)S(1)} %fusion.8, bf16[1536,2048]{1,0:T(8,128)(2,1)S(1)} %bitcast.57, bf16[1,2048,768]{2,1,0:T(8,128)(2,1)S(1)} %copy-done.3), kind=kOutput, calls=%fused_computation.4 | convolution fusion | flops 4838916096 | bytes 16515072 | tf_op jit(solution)/shard_map/dot_general | solution.py:45
  168.9 7.0 %convolution_convert_fusion = bf16[1536,2048]{1,0:T(8,128)(2,1)} fusion(bf16[1536,768]{1,0:T(8,128)(2,1)S(1)} %multiply_convert_fusion, bf16[1,768,2048]{2,1,0:T(8,128)(2,1)S(1)} %copy-done), kind=kOutput, calls=%fused_computation.1 | convolution fusion | flops 4834983936 | bytes 11796480 | tf_op jit(solution)/shard_map/dot_general | solution.py:47
  175.9 5.7 %all-to-all-start.1 = ((bf16[8,192,2048]{2,1,0:T(8,128)(2,1)}), bf16[8,192,2048]{2,1,0:T(8,128)(2,1)}, u32[]{:S(2)}, u32[]{:S(2)}) async-start(bf16[8,192,2048]{2,1,0:T(8,128)(2,1)} %bitcast.55), calls=%async_computation.1 | async-start | bytes 12582912 | tf_op jit(solution)/shard_map/all_to_all | solution.py:48
  181.6 71.3 %all-to-all-done.1 = bf16[8,192,2048]{2,1,0:T(8,128)(2,1)} async-done(((bf16[8,192,2048]{2,1,0:T(8,128)(2,1)}), bf16[8,192,2048]{2,1,0:T(8,128)(2,1)}, u32[]{:S(2)}, u32[]{:S(2)}) %all-to-all-start.1) | async-done | bytes 6291488 | tf_op jit(solution)/shard_map/all_to_all | solution.py:48
  252.8 6.1 %bitcast_convert_fusion = bf16[8,128,2048]{2,1,0:T(8,128)(2,1)} fusion(bf16[8,8,24,2048]{3,2,1,0:T(8,128)(2,1)} %bitcast.16, bf16[8,8,128]{2,0,1:T(8,128)(2,1)S(1)} %copy.36, bf16[8,8,128]{2,0,1:T(8,128)(2,1)S(1)} %copy.34), kind=kOutput, calls=%fused_computation | convolution fusion | flops 808189952 | bytes 10518528 | tf_op jit(solution)/shard_map/dslt,dslf->stf/dot_general | solution.py:52
  259.0 0.0 reduce-scatter.2.cloned.1.call-update
  259.6 51.8 %reduce-scatter.2.cloned.1.call-done = bf16[1,128,2048]{2,1,0:T(8,128)(2,1)} async-done(((bf16[8,128,2048]{2,1,0:T(8,128)(2,1)}), bf16[1,128,2048]{2,1,0:T(8,128)(2,1)}) %reduce-scatter.2.cloned.1.call-update) | async-done | bytes 524304 | tf_op jit(solution)/shard_map/reduce_scatter | solution.py:53
  311.5 2.2 fusion.11
  314.4 0.1 maximum_bitcast_fusion
  314.5 89.8 %all-gather.1 = f32[256,1,2]{2,1,0:T(1,128)S(1)} all-gather(f32[1,1,2]{2,1,0:T(1,128)S(1)} %maximum_bitcast_fusion), channel_id=1, replica_groups=mesh['x'=4,'z'=8,'core'=2,'dp'=4] {'x','z','core','dp'}, dimensions={0}, use_global_device_ids=true | all-gather | bytes 2056 | tf_op jit(solution)/shard_map/all_gather | solution.py:57
  404.3 0.2 slice_reduce_fusion.1
  404.5 0.1 select_reduce_fusion.2
  404.7 0.2 select_reduce_fusion.3
  404.8 0.6 pad_maximum_fusion
  (11 shorter events, 0.0 us)
Async XLA Ops:
  7.2 161.7 %copy-start = (bf16[1,768,2048]{2,1,0:T(8,128)(2,1)S(1)}, bf16[1,768,2048]{2,1,0:T(8,128)(2,1)}, u32[]{:S(2)}) copy-start(bf16[1,768,2048]{2,1,0:T(8,128)(2,1)} %param.13) | copy-start | bytes 9437188
  7.2 65.0 %all-gather.4.cloned.1.call-start = ((), (), s32[]{:S(2)}) async-start(), calls=%async_computation.4 | async-start | bytes 5013504 | tf_op jit(solution)/shard_map/all_gather | solution.py:26
  81.7 76.3 %copy-start.2 = (bf16[1,2048,768]{2,1,0:T(8,128)(2,1)S(1)}, bf16[1,2048,768]{2,1,0:T(8,128)(2,1)}, u32[]{:S(2)}) copy-start(bf16[1,2048,768]{2,1,0:T(8,128)(2,1)} %param.11) | copy-start | bytes 9437188
  158.0 5.2 %copy-start.3 = (bf16[1,2048,768]{2,1,0:T(8,128)(2,1)S(1)}, bf16[1,2048,768]{2,1,0:T(8,128)(2,1)}, u32[]{:S(2)}) copy-start(bf16[1,2048,768]{2,1,0:T(8,128)(2,1)} %param.12) | copy-start | bytes 9437188
  175.9 76.9 %all-to-all-start.1 = ((bf16[8,192,2048]{2,1,0:T(8,128)(2,1)}), bf16[8,192,2048]{2,1,0:T(8,128)(2,1)}, u32[]{:S(2)}, u32[]{:S(2)}) async-start(bf16[8,192,2048]{2,1,0:T(8,128)(2,1)} %bitcast.55), calls=%async_computation.1 | async-start | bytes 12582912 | tf_op jit(solution)/shard_map/all_to_all | solution.py:48
  181.6 129.9 %reduce-scatter.2.cloned.1.call-start = ((), (), s32[]{:S(2)}) async-start(), calls=%async_computation.3 | async-start | bytes 4718592 | tf_op jit(solution)/shard_map/reduce_scatter | solution.py:53
  252.8 58.6 %copy-start.1 = (f32[2048]{0:T(1024)S(1)}, f32[2048]{0:T(1024)}, u32[]{:S(2)}) copy-start(f32[2048]{0:T(1024)} %param.14) | copy-start | bytes 24580
Sparse Core Ops, SparseCore 0:
  11.3 60.8 all-gather.3
  259.1 52.2 reduce-scatter.1
where the time goes:
time: 413 us; the launch traced here: 412 us
  waiting for transfers between devices  184 us (45%)
  blocking collectives  166 us (40%)
  matrix products  30.4 us (7%)
  between operations  15.5 us (4%)
  local copies, waits for them, and re-layouts  7.92 us (2%)
  starting transfers between devices  5.71 us (1%)
    all_gather x1, blocking collectives, shards(): pairs = lax.all_gather(pair, EP_DP, tiled=True)  89.8 us
    all_to_all x1, blocking collectives, shards(): lax.all_to_all(send, ('x', 'core'), split_axis=0, concat_axis=0, tiled=True)  76.3 us
    all_to_all x1, waiting for transfers between devices, shards(): lax.all_to_all(result.reshape(recv.shape), ('x', 'core'), split_axis=0, c...  71.3 us
    all_gather x1, waiting for transfers between devices, shards(): held = lax.all_gather(packed, 'z')  61 us
    reduce_scatter x1, waiting for transfers between devices, shards(): lax.psum_scatter(part.astype(jnp.bfloat16), 'z', scatter_dimension=0, til...  51.8 us
  transfers between devices with their start and end apart: 3, of which 3 were waited for; matrix products, arithmetic and copies ran while one was open for 0% of the time, Pallas kernels for 0%

commit v1 on v0

--- a/solution.py
+++ b/solution.py
@@ -4,6 +4,7 @@
 from jax import lax
 from jax.sharding import Mesh
 from jax.sharding import PartitionSpec as P
+from jax.lax import all_to_all, axis_size
 
 TOP = 8
 PASSAGE = 128
@@ -54,7 +55,9 @@
     token_score = jnp.dot(mixed.astype(jnp.float32), score_head, precision=lax.Precision.HIGHEST)
     passage_score = token_score.reshape(-1, PASSAGE).sum(axis=1) / math.sqrt(PASSAGE)
     pair = jnp.stack([passage_score, doc_ids.astype(jnp.float32)], axis=1)
-    pairs = lax.all_gather(pair, EP_DP, tiled=True)
+    pairs = jnp.concatenate(
+        all_to_all(jnp.stack(axis_size(EP_DP) * [pair], axis=0), EP_DP, 0, 0), 0
+    )
     total = pairs.shape[0]
     docs = total // 4
     column = pairs[:, :1]

time: 413 us -> 346 us (0.84)
  blocking collectives: 166 us -> 99.4 us
    all_gather x1 -> x0, blocking collectives: 89.8 us -> none  [shards(): pairs = lax.all_gather(pair, EP_DP, tiled=True)]
    all_to_all x0 -> x1, blocking collectives: none -> 23.2 us  [shards(): all_to_all(jnp.stack(axis_size(EP_DP) * [pair], axis=0), EP_DP, 0, 0)]
where the time goes in v1:
time: 346 us
  waiting for transfers between devices  184 us (53%)
  blocking collectives  99.4 us (29%)
  matrix products  30.4 us (9%)
  between operations  15.5 us (4%)
  local copies, waits for them, and re-layouts  7.99 us (2%)
  starting transfers between devices  5.71 us (2%)
    all_to_all x1, blocking collectives, shards(): lax.all_to_all(send, ('x', 'core'), split_axis=0, concat_axis=0, tiled=True)  76.3 us
    all_to_all x1, waiting for transfers between devices, shards(): lax.all_to_all(result.reshape(recv.shape), ('x', 'core'), split_axis=0, c...  71.3 us
    all_gather x1, waiting for transfers between devices, shards(): held = lax.all_gather(packed, 'z')  61 us
    reduce_scatter x1, waiting for transfers between devices, shards(): lax.psum_scatter(part.astype(jnp.bfloat16), 'z', scatter_dimension=0, til...  51.8 us
    all_to_all x1, blocking collectives, shards(): all_to_all(jnp.stack(axis_size(EP_DP) * [pair], axis=0), EP_DP, 0, 0)  23.2 us
    dot_general x1, matrix products, shards(): jnp.dot(hidden, w_down[0], preferred_element_type=jnp.float32)  7.02 us
  transfers between devices with their start and end apart: 3, of which 3 were waited for; matrix products, arithmetic and copies ran while one was open for 0% of the time, Pallas kernels for 0%

profile of v1, /device:TPU:1, one launch (start us, length us, event | category | flops | bytes accessed | tf_op | source)
XLA Modules:
  0.0 345.7 jit_solution(7939566150697138938)
XLA Ops:
  7.2 0.0 all-gather.3.cloned.1.call-start
  7.2 0.9 fusion.14
  8.1 0.2 fusion.10
  8.3 0.1 copy.31
  8.5 0.7 fusion.19
  9.2 0.1 copy.32
  9.3 1.9 concatenate.3
  11.2 0.0 all-gather.3.cloned.1.call-update
  11.2 61.0 %all-gather.3.cloned.1.call-done = bf16[1024,2176]{1,0:T(8,128)(2,1)} async-done(((bf16[128,2176]{1,0:T(8,128)(2,1)}), bf16[1024,2176]{1,0:T(8,128)(2,1)}) %all-gather.3.cloned.1.call-update) | async-done | bytes 4456464 | tf_op jit(solution)/shard_map/all_gather | solution.py:27
  72.2 1.8 fusion.29
  74.0 1.1 copy.33
  75.1 0.8 copy.35
  75.9 0.7 constant_dynamic-slice_fusion
  76.6 4.0 %fusion.3 = bf16[8,8,24,2048]{3,2,0,1:T(8,128)(2,1)S(1)} fusion(bf16[8,128,2176]{2,1,0:T(8,128)(2,1)} %bitcast.66, bf16[8,8,128]{2,0,1:T(8,128)(2,1)S(1)} %copy.34), kind=kOutput, calls=%fused_computation.7 | convolution fusion | flops 805896192 | bytes 10502144 | tf_op jit(solution)/shard_map/dslt,stf->dslf/dot_general | solution.py:39
  80.6 1.1 copy.37
  81.7 76.3 %all_to_all.15 = bf16[8,192,2048]{2,1,0:T(8,128)(2,1)S(1)} all-to-all(bf16[8,192,2048]{2,1,0:T(8,128)(2,1)S(1)} %bitcast.54), channel_id=1, replica_groups=mesh['x'=4,'z'=8,'core'=2,'dp'=4] {'x','core'}, dimensions={0} | all-to-all | bytes 12582912 | tf_op jit(solution)/shard_map/all_to_all | solution.py:43
  158.0 5.2 %fusion.8 = f32[1536,768]{1,0:T(8,128)S(1)} fusion(bf16[1536,2048]{1,0:T(8,128)(2,1)S(1)} %bitcast.56, bf16[1,2048,768]{2,1,0:T(8,128)(2,1)S(1)} %copy-done.2), kind=kOutput, calls=%fused_computation.10 | convolution fusion | flops 4831838208 | bytes 14155776 | tf_op jit(solution)/shard_map/dot_general | solution.py:45
  163.2 5.6 %multiply_convert_fusion = bf16[1536,768]{1,0:T(8,128)(2,1)S(1)} fusion(f32[1536,768]{1,0:T(8,128)S(1)} %fusion.8, bf16[1536,2048]{1,0:T(8,128)(2,1)S(1)} %bitcast.57, bf16[1,2048,768]{2,1,0:T(8,128)(2,1)S(1)} %copy-done.3), kind=kOutput, calls=%fused_computation.4 | convolution fusion | flops 4838916096 | bytes 16515072 | tf_op jit(solution)/shard_map/dot_general | solution.py:46
  168.9 7.0 %convolution_convert_fusion = bf16[1536,2048]{1,0:T(8,128)(2,1)} fusion(bf16[1536,768]{1,0:T(8,128)(2,1)S(1)} %multiply_convert_fusion, bf16[1,768,2048]{2,1,0:T(8,128)(2,1)S(1)} %copy-done), kind=kOutput, calls=%fused_computation.1 | convolution fusion | flops 4834983936 | bytes 11796480 | tf_op jit(solution)/shard_map/dot_general | solution.py:48
  175.9 5.7 %all-to-all-start.1 = ((bf16[8,192,2048]{2,1,0:T(8,128)(2,1)}), bf16[8,192,2048]{2,1,0:T(8,128)(2,1)}, u32[]{:S(2)}, u32[]{:S(2)}) async-start(bf16[8,192,2048]{2,1,0:T(8,128)(2,1)} %bitcast.55), calls=%async_computation.1 | async-start | bytes 12582912 | tf_op jit(solution)/shard_map/all_to_all | solution.py:49
  181.6 71.3 %all-to-all-done.1 = bf16[8,192,2048]{2,1,0:T(8,128)(2,1)} async-done(((bf16[8,192,2048]{2,1,0:T(8,128)(2,1)}), bf16[8,192,2048]{2,1,0:T(8,128)(2,1)}, u32[]{:S(2)}, u32[]{:S(2)}) %all-to-all-start.1) | async-done | bytes 6291488 | tf_op jit(solution)/shard_map/all_to_all | solution.py:49
  252.8 6.1 %bitcast_convert_fusion = bf16[8,128,2048]{2,1,0:T(8,128)(2,1)} fusion(bf16[8,8,24,2048]{3,2,1,0:T(8,128)(2,1)} %bitcast.16, bf16[8,8,128]{2,0,1:T(8,128)(2,1)S(1)} %copy.36, bf16[8,8,128]{2,0,1:T(8,128)(2,1)S(1)} %copy.34), kind=kOutput, calls=%fused_computation | convolution fusion | flops 808189952 | bytes 10518528 | tf_op jit(solution)/shard_map/dslt,dslf->stf/dot_general | solution.py:53
  259.0 0.0 reduce-scatter.2.cloned.1.call-update
  259.6 51.8 %reduce-scatter.2.cloned.1.call-done = bf16[1,128,2048]{2,1,0:T(8,128)(2,1)} async-done(((bf16[8,128,2048]{2,1,0:T(8,128)(2,1)}), bf16[1,128,2048]{2,1,0:T(8,128)(2,1)}) %reduce-scatter.2.cloned.1.call-update) | async-done | bytes 524304 | tf_op jit(solution)/shard_map/reduce_scatter | solution.py:54
  311.5 2.2 fusion.11
  314.4 0.1 maximum_bitcast_fusion
  314.5 0.1 stack.22
  314.6 23.2 %all_to_all.16 = f32[256,1,2]{2,1,0:T(1,128)S(1)} all-to-all(f32[256,1,2]{2,1,0:T(1,128)S(1)} %stack.22), channel_id=1, replica_groups=mesh['x'=4,'z'=8,'core'=2,'dp'=4] {'x','z','core','dp'}, dimensions={0} | all-to-all | bytes 4096 | tf_op jit(solution)/shard_map/all_to_all | solution.py:59
  337.7 0.2 slice_reduce_fusion.1
  338.0 0.1 select_reduce_fusion.2
  338.1 0.2 select_reduce_fusion.3
  338.3 0.6 pad_maximum_fusion
  (12 shorter events, 0.0 us)
Async XLA Ops:
  7.2 161.7 %copy-start = (bf16[1,768,2048]{2,1,0:T(8,128)(2,1)S(1)}, bf16[1,768,2048]{2,1,0:T(8,128)(2,1)}, u32[]{:S(2)}) copy-start(bf16[1,768,2048]{2,1,0:T(8,128)(2,1)} %param.13) | copy-start | bytes 9437188
  7.2 65.0 %all-gather.3.cloned.1.call-start = ((), (), s32[]{:S(2)}) async-start(), calls=%async_computation.5 | async-start | bytes 5013504 | tf_op jit(solution)/shard_map/all_gather | solution.py:27
  81.7 76.3 %copy-start.2 = (bf16[1,2048,768]{2,1,0:T(8,128)(2,1)S(1)}, bf16[1,2048,768]{2,1,0:T(8,128)(2,1)}, u32[]{:S(2)}) copy-start(bf16[1,2048,768]{2,1,0:T(8,128)(2,1)} %param.11) | copy-start | bytes 9437188
  158.0 5.2 %copy-start.3 = (bf16[1,2048,768]{2,1,0:T(8,128)(2,1)S(1)}, bf16[1,2048,768]{2,1,0:T(8,128)(2,1)}, u32[]{:S(2)}) copy-start(bf16[1,2048,768]{2,1,0:T(8,128)(2,1)} %param.12) | copy-start | bytes 9437188
  175.9 76.9 %all-to-all-start.1 = ((bf16[8,192,2048]{2,1,0:T(8,128)(2,1)}), bf16[8,192,2048]{2,1,0:T(8,128)(2,1)}, u32[]{:S(2)}, u32[]{:S(2)}) async-start(bf16[8,192,2048]{2,1,0:T(8,128)(2,1)} %bitcast.55), calls=%async_computation.1 | async-start | bytes 12582912 | tf_op jit(solution)/shard_map/all_to_all | solution.py:49
  181.6 129.9 %reduce-scatter.2.cloned.1.call-start = ((), (), s32[]{:S(2)}) async-start(), calls=%async_computation.4 | async-start | bytes 4718592 | tf_op jit(solution)/shard_map/reduce_scatter | solution.py:54
  252.8 58.6 %copy-start.1 = (f32[2048]{0:T(1024)S(1)}, f32[2048]{0:T(1024)}, u32[]{:S(2)}) copy-start(f32[2048]{0:T(1024)} %param.14) | copy-start | bytes 24580
Sparse Core Ops, SparseCore 0:
  11.3 60.8 all-gather.2
  259.1 52.2 reduce-scatter.1
